TPU v7x, 32 devices: a whole 2x2x4 slice. The times are simulated.
32 devices in a mesh: row: 4 (over y, core), col: 8 (over z, x).
Axes of the slice: x: 2, y: 2, z: 4, core: 2. Of those that a mesh axis runs over, the one named last changes fastest.
Arguments:
- first_acts: bfloat16 [2048, 18944], P('col', 'row'), may hold values from -320 to 320, as said below
- second_acts: bfloat16 [2048, 18944], P('row', 'col'), may hold values from -320 to 320, as said below
Outputs:
- row_potential: float32 [18944], P('row')
- column_potential: float32 [18944], P('col')
Inputs may be any that keep to these rules, and one draw needn't show every extreme that they name: `first_acts`: real-valued activations. `second_acts`: real-valued activations.
All inputs are finite; a program needn't handle non-finite values.
Results may differ from a plain program's by a relative error of at most 0.0003.
Values may be sent and summed in bfloat16 or wider, within the bound.
A program may use at most 128 MiB of HBM per device.

v0:
```python
import math
import jax
import jax.numpy as jnp
from jax import lax
from jax.sharding import PartitionSpec as P

NEUR = 18944
SAMP = 2048
ITERS = 4
entropy_scale = 0.004


def row_lse(scores, log_share):
    highest = jnp.max(scores, 1)
    totals = jnp.sum(jnp.exp(scores - highest[:, None]), 1)
    members = lax.axis_size("col")
    maxima, sums = (
        lax.all_to_all(
            highest.reshape(members, -1), "col", split_axis=0, concat_axis=0, tiled=True
        ),
        lax.all_to_all(totals.reshape(members, -1), "col", split_axis=0, concat_axis=0, tiled=True),
    )
    overall = jnp.max(maxima, 0)
    merged_sum = jnp.sum(sums * jnp.exp(maxima - overall[None, :]), 0)
    own_part = log_share - (overall + jnp.log(merged_sum))
    return lax.all_gather(own_part, "col", axis=0, tiled=True)


def col_lse(scores, log_share):
    highest = jnp.max(scores, 0)
    totals = jnp.sum(jnp.exp(scores - highest[None, :]), 0)
    members = lax.axis_size("row")
    maxima, sums = (
        lax.all_to_all(
            highest.reshape(members, -1), "row", split_axis=0, concat_axis=0, tiled=True
        ),
        lax.all_to_all(totals.reshape(members, -1), "row", split_axis=0, concat_axis=0, tiled=True),
    )
    overall = jnp.max(maxima, 0)
    merged_sum = jnp.sum(sums * jnp.exp(maxima - overall[None, :]), 0)
    own_part = log_share - (overall + jnp.log(merged_sum))
    return lax.all_gather(own_part, "row", axis=0, tiled=True)


def shards(first_acts, second_acts):
    full_second = lax.all_gather(second_acts, "row", axis=0, tiled=True)
    rows_here = first_acts.shape[1]
    cols_here = second_acts.shape[1]
    segment = lax.all_gather(first_acts, "col", axis=0, tiled=True)
    products = lax.dot_general(
        segment, full_second, (((0,), (0,)), ((), ())), preferred_element_type=jnp.float32
    )
    widened = segment.astype(jnp.float32)
    products, first_squares = (products, jnp.sum(widened * widened, 0))
    second_wide = full_second.astype(jnp.float32)
    second_squares = jnp.sum(second_wide * second_wide, 0)
    inv_first = 1.0 / jnp.sqrt(first_squares / SAMP + 1e-06)
    inv_second = 1.0 / jnp.sqrt(second_squares / SAMP + 1e-06)
    logk = products * inv_first[:, None] * inv_second[None, :] * (1.0 / (SAMP * entropy_scale))
    log_share = -math.log(NEUR)
    row_potential = jnp.zeros((rows_here,), jnp.float32)
    column_potential = jnp.zeros((cols_here,), jnp.float32)
    for step in range(ITERS):
        row_potential = row_lse(column_potential[None, :] + logk, log_share)
        column_potential = col_lse(row_potential[:, None] + logk, log_share)
    return (row_potential, column_potential)


def solution(mesh):
    return jax.shard_map(
        shards,
        mesh=mesh,
        in_specs=(P("col", "row"), P("row", "col")),
        out_specs=(P("row"), P("col")),
        check_vma=False,
    )
```

profile of v0, /device:TPU:0, one launch (start us, length us, event | category | flops | bytes accessed | tf_op | source)
XLA Modules:
  0.0 1064.9 jit_solution(205873519118053908)
XLA Ops:
  8.6 69.4 %all-gather.5.cloned.1.call-done = bf16[2048,2368]{0,1:T(8,128)(2,1)} async-done(((bf16[512,2368]{0,1:T(8,128)(2,1)}), bf16[2048,2368]{0,1:T(8,128)(2,1)}) %all-gather.5.cloned.1.call-update) | async-done | bytes 9699344 | tf_op jit(solution)/shard_map/all_gather | solution.py:46
  83.7 368.1 %all-gather.3.cloned.1.call-done = bf16[2048,4736]{1,0:T(8,128)(2,1)} async-done(((bf16[256,4736]{1,0:T(8,128)(2,1)}), bf16[2048,4736]{1,0:T(8,128)(2,1)}) %all-gather.3.cloned.1.call-update) | async-done | bytes 19398672 | tf_op jit(solution)/shard_map/all_gather | solution.py:49
  451.8 8.4 multiply_reduce_fusion
  460.2 59.7 %fusion.24 = (f32[4736]{0:T(1024)S(1)}, f32[4736,2368]{0,1:T(8,128)}) fusion(f32[2368]{0:T(1024)S(1)} %add_rsqrt_fusion.1, f32[4736]{0:T(1024)S(1)} %add_rsqrt_fusion, bf16[2048,2368]{0,1:T(8,128)(2,1)} %all-gather.5.cloned.1.call-done, bf16[2048,4736]{1,0:T(8,128)(2,1)} %all-gather.3.cloned.1.call-done), kind=kOutput, calls=%fused_computation.60 | convolution fusion | flops 45980872704 | bytes 74004736 | tf_op jit(solution)/shard_map/dot_general | solution.py:50
  525.2 17.3 %exponential_reduce_fusion.7 = f32[4736]{0:T(1024)S(1)} fusion(f32[4736,2368]{0,1:T(8,128)} %get-tuple-element.3, f32[4736]{0:T(1024)S(1)} %get-tuple-element.2), kind=kLoop, calls=%fused_computation.7 | loop fusion | flops 22424960 | bytes 44897280 | tf_op jit(solution)/shard_map/reduce_sum | solution.py:15
  543.3 6.0 all-to-all-start.1
  556.0 33.5 %all-reduce = f32[4736]{0:T(1024)S(1)} all-reduce(f32[4736]{0:T(1024)S(1)} %subtract_dynamic-update-slice_fusion.7), channel_id=1, replica_groups=mesh['row'=4,'col'=8] {'col'}, use_global_device_ids=true, to_apply=%add | all-reduce | flops 4736 | bytes 37888
  589.5 14.8 %add_reduce_fusion.6 = f32[2368]{0:T(1024)S(1)} fusion(f32[4736,2368]{0,1:T(8,128)} %get-tuple-element.3, f32[4736]{0:T(1024)S(1)} %all-reduce), kind=kLoop, calls=%fused_computation.15 | loop fusion | flops 22427328 | bytes 44887808 | tf_op jit(solution)/shard_map/reduce_max | solution.py:30
  608.2 15.9 %exponential_reduce_fusion.6 = f32[2368]{0:T(1024)S(1)} fusion(f32[4736,2368]{0,1:T(8,128)} %get-tuple-element.3, f32[2368]{0:T(1024)S(1)} %add_reduce_fusion.6, f32[4736]{0:T(1024)S(1)} %all-reduce), kind=kLoop, calls=%fused_computation.6 | loop fusion | flops 33642176 | bytes 44897280 | tf_op jit(solution)/shard_map/reduce_sum | solution.py:31
  632.0 10.1 all-reduce.1
  642.1 16.4 %add_reduce_fusion.5 = f32[4736]{0:T(1024)S(1)} fusion(f32[4736,2368]{0,1:T(8,128)} %get-tuple-element.3, f32[2368]{0:T(1024)S(1)} %all-reduce.1), kind=kLoop, calls=%fused_computation.14 | loop fusion | flops 22424960 | bytes 44887808 | tf_op jit(solution)/shard_map/reduce_max | solution.py:14
  662.6 18.4 %exponential_reduce_fusion.5 = f32[4736]{0:T(1024)S(1)} fusion(f32[4736,2368]{0,1:T(8,128)} %get-tuple-element.3, f32[4736]{0:T(1024)S(1)} %add_reduce_fusion.5, f32[2368]{0:T(1024)S(1)} %all-reduce.1), kind=kLoop, calls=%fused_computation.5 | loop fusion | flops 33639808 | bytes 44906752 | tf_op jit(solution)/shard_map/reduce_sum | solution.py:15
  681.7 5.9 all-to-all-start.5
  687.7 6.6 all-to-all-done.5
  694.4 33.5 %all-reduce.2 = f32[4736]{0:T(1024)S(1)} all-reduce(f32[4736]{0:T(1024)S(1)} %subtract_dynamic-update-slice_fusion.5), channel_id=1, replica_groups=mesh['row'=4,'col'=8] {'col'}, use_global_device_ids=true, to_apply=%add.2 | all-reduce | flops 4736 | bytes 37888
  727.9 14.8 %add_reduce_fusion.4 = f32[2368]{0:T(1024)S(1)} fusion(f32[4736,2368]{0,1:T(8,128)} %get-tuple-element.3, f32[4736]{0:T(1024)S(1)} %all-reduce.2), kind=kLoop, calls=%fused_computation.13 | loop fusion | flops 22427328 | bytes 44887808 | tf_op jit(solution)/shard_map/reduce_max | solution.py:30
  746.6 15.9 %exponential_reduce_fusion.4 = f32[2368]{0:T(1024)S(1)} fusion(f32[4736,2368]{0,1:T(8,128)} %get-tuple-element.3, f32[2368]{0:T(1024)S(1)} %add_reduce_fusion.4, f32[4736]{0:T(1024)S(1)} %all-reduce.2), kind=kLoop, calls=%fused_computation.4 | loop fusion | flops 33642176 | bytes 44897280 | tf_op jit(solution)/shard_map/reduce_sum | solution.py:31
  770.4 10.1 all-reduce.3
  780.5 16.4 %add_reduce_fusion.3 = f32[4736]{0:T(1024)S(1)} fusion(f32[4736,2368]{0,1:T(8,128)} %get-tuple-element.3, f32[2368]{0:T(1024)S(1)} %all-reduce.3), kind=kLoop, calls=%fused_computation.12 | loop fusion | flops 22424960 | bytes 44887808 | tf_op jit(solution)/shard_map/reduce_max | solution.py:14
  801.0 18.4 %exponential_reduce_fusion.3 = f32[4736]{0:T(1024)S(1)} fusion(f32[4736,2368]{0,1:T(8,128)} %get-tuple-element.3, f32[4736]{0:T(1024)S(1)} %add_reduce_fusion.3, f32[2368]{0:T(1024)S(1)} %all-reduce.3), kind=kLoop, calls=%fused_computation.3 | loop fusion | flops 33639808 | bytes 44906752 | tf_op jit(solution)/shard_map/reduce_sum | solution.py:15
  826.0 6.6 all-to-all-done.9
  832.8 33.5 %all-reduce.4 = f32[4736]{0:T(1024)S(1)} all-reduce(f32[4736]{0:T(1024)S(1)} %subtract_dynamic-update-slice_fusion.3), channel_id=1, replica_groups=mesh['row'=4,'col'=8] {'col'}, use_global_device_ids=true, to_apply=%add.4 | all-reduce | flops 4736 | bytes 37888
  866.2 14.8 %add_reduce_fusion.2 = f32[2368]{0:T(1024)S(1)} fusion(f32[4736,2368]{0,1:T(8,128)} %get-tuple-element.3, f32[4736]{0:T(1024)S(1)} %all-reduce.4), kind=kLoop, calls=%fused_computation.11 | loop fusion | flops 22427328 | bytes 44887808 | tf_op jit(solution)/shard_map/reduce_max | solution.py:30
  885.2 15.9 %exponential_reduce_fusion.2 = f32[2368]{0:T(1024)S(1)} fusion(f32[4736,2368]{0,1:T(8,128)} %get-tuple-element.3, f32[2368]{0:T(1024)S(1)} %add_reduce_fusion.2, f32[4736]{0:T(1024)S(1)} %all-reduce.4), kind=kLoop, calls=%fused_computation.2 | loop fusion | flops 33642176 | bytes 44897280 | tf_op jit(solution)/shard_map/reduce_sum | solution.py:31
  908.9 10.1 all-reduce.5
  919.0 16.4 %add_reduce_fusion.1 = f32[4736]{0:T(1024)S(1)} fusion(f32[4736,2368]{0,1:T(8,128)} %get-tuple-element.3, f32[2368]{0:T(1024)S(1)} %all-reduce.5), kind=kLoop, calls=%fused_computation.10 | loop fusion | flops 22424960 | bytes 44887808 | tf_op jit(solution)/shard_map/reduce_max | solution.py:14
  939.5 18.4 %exponential_reduce_fusion.1 = f32[4736]{0:T(1024)S(1)} fusion(f32[4736,2368]{0,1:T(8,128)} %get-tuple-element.3, f32[4736]{0:T(1024)S(1)} %add_reduce_fusion.1, f32[2368]{0:T(1024)S(1)} %all-reduce.5), kind=kLoop, calls=%fused_computation.1 | loop fusion | flops 33639808 | bytes 44906752 | tf_op jit(solution)/shard_map/reduce_sum | solution.py:15
  964.6 6.6 all-to-all-done.13
  971.3 33.5 %all-reduce.6 = f32[4736]{0:T(1024)S(1)} all-reduce(f32[4736]{0:T(1024)S(1)} %subtract_dynamic-update-slice_fusion.1), channel_id=1, replica_groups=mesh['row'=4,'col'=8] {'col'}, use_global_device_ids=true, to_apply=%add.6 | all-reduce | flops 4736 | bytes 37888
  1004.8 14.8 %add_reduce_fusion = f32[2368]{0:T(1024)S(1)} fusion(f32[4736,2368]{0,1:T(8,128)} %get-tuple-element.3, f32[4736]{0:T(1024)S(1)} %all-reduce.6), kind=kLoop, calls=%fused_computation.9 | loop fusion | flops 22427328 | bytes 44887808 | tf_op jit(solution)/shard_map/reduce_max | solution.py:30
  1023.5 15.9 %exponential_reduce_fusion = f32[2368]{0:T(1024)S(1)} fusion(f32[4736,2368]{0,1:T(8,128)} %get-tuple-element.3, f32[2368]{0:T(1024)S(1)} %add_reduce_fusion, f32[4736]{0:T(1024)S(1)} %all-reduce.6), kind=kLoop, calls=%fused_computation | loop fusion | flops 33642176 | bytes 44897280 | tf_op jit(solution)/shard_map/reduce_sum | solution.py:31
  1047.3 10.7 %all-reduce.7 = f32[2368]{0:T(1024)} all-reduce(f32[2368]{0:T(1024)S(1)} %subtract_dynamic-update-slice_fusion), channel_id=1, replica_groups=mesh['row'=4,'col'=8] {'row'}, use_global_device_ids=true, to_apply=%add.7 | all-reduce | flops 2368 | bytes 18944
  (90 shorter events, 92.7 us)
Async XLA Ops:
  7.2 70.8 %all-gather.5.cloned.1.call-start = ((), (), s32[]{:S(2)}) async-start(), calls=%async_computation.17 | async-start | bytes 12124160 | tf_op jit(solution)/shard_map/all_gather | solution.py:46
  7.9 443.9 %all-gather.3.cloned.1.call-start = ((), (), s32[]{:S(2)}) async-start(), calls=%async_computation.16 | async-start | bytes 21823488 | tf_op jit(solution)/shard_map/all_gather | solution.py:49
  519.9 29.3 %copy-start.2 = (u32[32]{0:T(128)S(1)}, u32[32]{0:T(128)}, u32[]{:S(2)}) copy-start(u32[32]{0:T(128)} %constant.20) | copy-start | bytes 388
  520.6 22.6 %all-to-all-start = ((f32[8,1,592]{2,1,0:T(1,128)}), f32[8,1,592]{2,1,0:T(1,128)S(1)}, u32[]{:S(2)}, u32[]{:S(2)}) async-start(f32[8,1,592]{2,1,0:T(1,128)} %all_to_all.128), calls=%async_computation | async-start | bytes 40960 | tf_op jit(solution)/shard_map/all_to_all | solution.py:18
  543.3 12.6 %all-to-all-start.1 = ((f32[8,1,592]{2,1,0:T(1,128)}), f32[8,1,592]{2,1,0:T(1,128)S(1)}, u32[]{:S(2)}, u32[]{:S(2)}) async-start(f32[8,1,592]{2,1,0:T(1,128)} %all_to_all.130), calls=%async_computation.1 | async-start | bytes 40960 | tf_op jit(solution)/shard_map/all_to_all | solution.py:21
  589.5 38.5 %copy-start.1 = (u32[32]{0:T(128)S(1)}, u32[32]{0:T(128)}, u32[]{:S(2)}) copy-start(u32[32]{0:T(128)} %constant.25) | copy-start | bytes 388
  605.0 19.8 %all-to-all-start.2 = ((f32[4,1,592]{2,1,0:T(1,128)}), f32[4,1,592]{2,1,0:T(1,128)S(1)}, u32[]{:S(2)}, u32[]{:S(2)}) async-start(f32[4,1,592]{2,1,0:T(1,128)} %all_to_all.134), calls=%async_computation.2 | async-start | bytes 20480 | tf_op jit(solution)/shard_map/all_to_all | solution.py:34
  624.8 7.1 all-to-all-start.3
  659.3 22.5 %all-to-all-start.4 = ((f32[8,1,592]{2,1,0:T(1,128)}), f32[8,1,592]{2,1,0:T(1,128)S(1)}, u32[]{:S(2)}, u32[]{:S(2)}) async-start(f32[8,1,592]{2,1,0:T(1,128)} %all_to_all.140), calls=%async_computation.4 | async-start | bytes 40960 | tf_op jit(solution)/shard_map/all_to_all | solution.py:18
  681.7 12.5 %all-to-all-start.5 = ((f32[8,1,592]{2,1,0:T(1,128)}), f32[8,1,592]{2,1,0:T(1,128)S(1)}, u32[]{:S(2)}, u32[]{:S(2)}) async-start(f32[8,1,592]{2,1,0:T(1,128)} %all_to_all.142), calls=%async_computation.5 | async-start | bytes 40960 | tf_op jit(solution)/shard_map/all_to_all | solution.py:21
  743.3 19.8 %all-to-all-start.6 = ((f32[4,1,592]{2,1,0:T(1,128)}), f32[4,1,592]{2,1,0:T(1,128)S(1)}, u32[]{:S(2)}, u32[]{:S(2)}) async-start(f32[4,1,592]{2,1,0:T(1,128)} %all_to_all.146), calls=%async_computation.6 | async-start | bytes 20480 | tf_op jit(solution)/shard_map/all_to_all | solution.py:34
  763.1 7.1 all-to-all-start.7
  797.6 22.5 %all-to-all-start.8 = ((f32[8,1,592]{2,1,0:T(1,128)}), f32[8,1,592]{2,1,0:T(1,128)S(1)}, u32[]{:S(2)}, u32[]{:S(2)}) async-start(f32[8,1,592]{2,1,0:T(1,128)} %all_to_all.152), calls=%async_computation.8 | async-start | bytes 40960 | tf_op jit(solution)/shard_map/all_to_all | solution.py:18
  820.1 12.5 %all-to-all-start.9 = ((f32[8,1,592]{2,1,0:T(1,128)}), f32[8,1,592]{2,1,0:T(1,128)S(1)}, u32[]{:S(2)}, u32[]{:S(2)}) async-start(f32[8,1,592]{2,1,0:T(1,128)} %all_to_all.154), calls=%async_computation.9 | async-start | bytes 40960 | tf_op jit(solution)/shard_map/all_to_all | solution.py:21
  881.7 20.0 %all-to-all-start.10 = ((f32[4,1,592]{2,1,0:T(1,128)}), f32[4,1,592]{2,1,0:T(1,128)S(1)}, u32[]{:S(2)}, u32[]{:S(2)}) async-start(f32[4,1,592]{2,1,0:T(1,128)} %all_to_all.158), calls=%async_computation.10 | async-start | bytes 20480 | tf_op jit(solution)/shard_map/all_to_all | solution.py:34
  901.7 7.0 all-to-all-start.11
  936.2 22.5 %all-to-all-start.12 = ((f32[8,1,592]{2,1,0:T(1,128)}), f32[8,1,592]{2,1,0:T(1,128)S(1)}, u32[]{:S(2)}, u32[]{:S(2)}) async-start(f32[8,1,592]{2,1,0:T(1,128)} %all_to_all.164), calls=%async_computation.12 | async-start | bytes 40960 | tf_op jit(solution)/shard_map/all_to_all | solution.py:18
  958.6 12.5 %all-to-all-start.13 = ((f32[8,1,592]{2,1,0:T(1,128)}), f32[8,1,592]{2,1,0:T(1,128)S(1)}, u32[]{:S(2)}, u32[]{:S(2)}) async-start(f32[8,1,592]{2,1,0:T(1,128)} %all_to_all.166), calls=%async_computation.13 | async-start | bytes 40960 | tf_op jit(solution)/shard_map/all_to_all | solution.py:21
  1004.8 34.6 %copy-start = (f32[4736]{0:T(1024)}, f32[4736]{0:T(1024)S(1)}, u32[]{:S(2)}) copy-start(f32[4736]{0:T(1024)S(1)} %all-reduce.6) | copy-start | bytes 56836
  1020.3 19.8 %all-to-all-start.14 = ((f32[4,1,592]{2,1,0:T(1,128)}), f32[4,1,592]{2,1,0:T(1,128)S(1)}, u32[]{:S(2)}, u32[]{:S(2)}) async-start(f32[4,1,592]{2,1,0:T(1,128)} %all_to_all.170), calls=%async_computation.14 | async-start | bytes 20480 | tf_op jit(solution)/shard_map/all_to_all | solution.py:34
  1040.1 7.1 all-to-all-start.15
Sparse Core Ops, SparseCore 0:
  9.5 68.4 all-gather.4
  79.5 372.2 all-gather.2
where the time goes:
time: 1070 us; the launch traced here: 1060 us
  waiting for transfers between devices  478 us (45%)
  other arithmetic  260 us (24%)
  blocking collectives  175 us (16%)
  starting transfers between devices  64.7 us (6%)
  matrix products  59.7 us (6%)
  between operations  15.7 us (1%)
  local copies, waits for them, and re-layouts  12.3 us (1%)
    all_gather x1, waiting for transfers between devices, shards(): segment = lax.all_gather(first_acts, 'col', axis=0, tiled=True)  368 us
    unnamed x8, blocking collectives  175 us
    reduce_sum x4, other arithmetic, row_lse(): totals = jnp.sum(jnp.exp(scores - highest[:, None]), 1)  72.5 us
    all_gather x1, waiting for transfers between devices, shards(): full_second = lax.all_gather(second_acts, 'row', axis=0, tiled=True)  69.4 us
    reduce_sum x4, other arithmetic, col_lse(): totals = jnp.sum(jnp.exp(scores - highest[None, :]), 0)  63.5 us
    dot_general x1, matrix products, shards(): lax.dot_general(segment, full_second, (((0,), (0,)), ((), ())), preferred...  59.7 us
    reduce_max x4, other arithmetic, col_lse(): highest = jnp.max(scores, 0)  59.1 us
    reduce_max x3, other arithmetic, row_lse(): highest = jnp.max(scores, 1)  49.3 us
  transfers between devices with their start and end apart: 18, of which 10 were waited for; matrix products, arithmetic and copies ran while one was open for 13% of the time, Pallas kernels for 0%

commit v1 on v0

--- a/solution.py
+++ b/solution.py
@@ -43,7 +43,12 @@
 
 
 def shards(first_acts, second_acts):
-    full_second = lax.all_gather(second_acts, "row", axis=0, tiled=True)
+    ring = [second_acts]
+    for hop in range(3):
+        ring.append(lax.ppermute(ring[-1], "row", [(dev, (dev + 1) % 4) for dev in range(4)]))
+    full_second = jnp.roll(
+        jnp.concatenate(ring[::-1], axis=0), (lax.axis_index("row") + 1) * ring[0].shape[0], axis=0
+    )
     rows_here = first_acts.shape[1]
     cols_here = second_acts.shape[1]
     segment = lax.all_gather(first_acts, "col", axis=0, tiled=True)

time: 1070 us -> 1000 us (0.935)
  waiting for transfers between devices: 478 us -> 386 us
  local copies, waits for them, and re-layouts: 12.3 us -> 35.7 us
    all_gather x1, waiting for transfers between devices: 368 us -> 259 us  [shards(): segment = lax.all_gather(first_acts, 'col', axis=0, tiled=True)]
    ppermute x0 -> x3, waiting for transfers between devices: none -> 87.7 us  [shards(): lax.ppermute(ring[-1], 'row', [(dev, (dev + 1) % 4) for dev in range(4)])]
    all_gather x1 -> x0, waiting for transfers between devices: 69.4 us -> none  [shards(): full_second = lax.all_gather(second_acts, 'row', axis=0, tiled=True)]
    unnamed x16 -> x23, local copies, waits for them, and re-layouts: 1.21 us -> 21.3 us
  transfers between devices with their start and end apart: 18 -> 20, of which waited for: 10 -> 12; matrix products, arithmetic and copies ran while one was open for 13% -> 17% of each run, Pallas kernels for 0% -> 0%
where the time goes in v1:
time: 1000 us; the launch traced here: 998 us
  waiting for transfers between devices  386 us (39%)
  other arithmetic  260 us (26%)
  blocking collectives  175 us (18%)
  starting transfers between devices  65.2 us (7%)
  matrix products  59.8 us (6%)
  local copies, waits for them, and re-layouts  35.7 us (4%)
  between operations  15.7 us (2%)
    all_gather x1, waiting for transfers between devices, shards(): segment = lax.all_gather(first_acts, 'col', axis=0, tiled=True)  259 us
    unnamed x8, blocking collectives  175 us
    ppermute x3, waiting for transfers between devices, shards(): lax.ppermute(ring[-1], 'row', [(dev, (dev + 1) % 4) for dev in range(4)])  87.7 us
    reduce_sum x4, other arithmetic, row_lse(): totals = jnp.sum(jnp.exp(scores - highest[:, None]), 1)  72.5 us
    reduce_sum x4, other arithmetic, col_lse(): totals = jnp.sum(jnp.exp(scores - highest[None, :]), 0)  63.5 us
    dot_general x1, matrix products, shards(): lax.dot_general(segment, full_second, (((0,), (0,)), ((), ())), preferred...  59.8 us
    reduce_max x4, other arithmetic, col_lse(): highest = jnp.max(scores, 0)  59.1 us
    reduce_max x3, other arithmetic, row_lse(): highest = jnp.max(scores, 1)  49.3 us
  transfers between devices with their start and end apart: 20, of which 12 were waited for; matrix products, arithmetic and copies ran while one was open for 17% of the time, Pallas kernels for 0%

profile of v1, /device:TPU:0, one launch (start us, length us, event | category | flops | bytes accessed | tf_op | source)
XLA Modules:
  0.0 997.6 jit_solution(18200518527465197740)
XLA Ops:
  8.4 29.4 %collective-permute-done = bf16[512,2368]{0,1:T(8,128)(2,1)S(1)} collective-permute-done((bf16[512,2368]{0,1:T(8,128)(2,1)}, bf16[512,2368]{0,1:T(8,128)(2,1)S(1)}, u32[]{:S(2)}, u32[]{:S(2)}) %collective-permute-start) | collective-permute-done | bytes 2424864 | tf_op jit(solution)/shard_map/ppermute | solution.py:48
  37.9 29.0 %collective-permute-done.1 = bf16[512,2368]{0,1:T(8,128)(2,1)} collective-permute-done((bf16[512,2368]{0,1:T(8,128)(2,1)S(1)}, bf16[512,2368]{0,1:T(8,128)(2,1)}, u32[]{:S(2)}, u32[]{:S(2)}) %collective-permute-start.1) | collective-permute-done | bytes 2424864 | tf_op jit(solution)/shard_map/ppermute | solution.py:48
  66.9 29.3 %collective-permute-done.2 = bf16[512,2368]{0,1:T(8,128)(2,1)} collective-permute-done((bf16[512,2368]{0,1:T(8,128)(2,1)}, bf16[512,2368]{0,1:T(8,128)(2,1)}, u32[]{:S(2)}, u32[]{:S(2)}) %collective-permute-start.2) | collective-permute-done | bytes 2424864 | tf_op jit(solution)/shard_map/ppermute | solution.py:48
  125.4 259.0 %all-gather.2.cloned.1.call-done = bf16[2048,4736]{1,0:T(8,128)(2,1)} async-done(((bf16[256,4736]{1,0:T(8,128)(2,1)}), bf16[2048,4736]{1,0:T(8,128)(2,1)}) %all-gather.2.cloned.1.call-update) | async-done | bytes 19398672 | tf_op jit(solution)/shard_map/all_gather | solution.py:54
  384.5 8.4 multiply_reduce_fusion
  392.9 59.8 %fusion.26 = (f32[4736]{0:T(1024)S(1)}, f32[2368,4736]{1,0:T(8,128)}) fusion(f32[2368]{0:T(1024)S(1)} %add_rsqrt_fusion.1, f32[4736]{0:T(1024)S(1)} %add_rsqrt_fusion, bf16[2048,4736]{1,0:T(8,128)(2,1)} %all-gather.2.cloned.1.call-done, bf16[4096,2368]{0,1:T(8,128)(2,1)} %constant_dynamic-update-slice_fusion, s32[]{:T(128)S(6)} %select_n.14), kind=kOutput, calls=%fused_computation.70 | convolution fusion | flops 45980872704 | bytes 74004736 | tf_op jit(solution)/shard_map/dot_general | solution.py:55
  457.9 17.3 %exponential_reduce_fusion.7 = f32[4736]{0:T(1024)S(1)} fusion(f32[2368,4736]{1,0:T(8,128)} %get-tuple-element.3, f32[4736]{0:T(1024)S(1)} %get-tuple-element.2), kind=kLoop, calls=%fused_computation.7 | loop fusion | flops 22424960 | bytes 44897280 | tf_op jit(solution)/shard_map/reduce_sum | solution.py:15
  488.7 33.5 %all-reduce = f32[4736]{0:T(1024)S(1)} all-reduce(f32[4736]{0:T(1024)S(1)} %subtract_dynamic-update-slice_fusion.7), channel_id=1, replica_groups=mesh['row'=4,'col'=8] {'col'}, use_global_device_ids=true, to_apply=%add | all-reduce | flops 4736 | bytes 37888
  522.2 14.8 %add_reduce_fusion.6 = f32[2368]{0:T(1024)S(1)} fusion(f32[2368,4736]{1,0:T(8,128)} %get-tuple-element.3, f32[4736]{0:T(1024)S(1)} %all-reduce), kind=kLoop, calls=%fused_computation.15 | loop fusion | flops 22427328 | bytes 44887808 | tf_op jit(solution)/shard_map/reduce_max | solution.py:30
  541.1 15.9 %exponential_reduce_fusion.6 = f32[2368]{0:T(1024)S(1)} fusion(f32[2368,4736]{1,0:T(8,128)} %get-tuple-element.3, f32[2368]{0:T(1024)S(1)} %add_reduce_fusion.6, f32[4736]{0:T(1024)S(1)} %all-reduce), kind=kLoop, calls=%fused_computation.6 | loop fusion | flops 33642176 | bytes 44897280 | tf_op jit(solution)/shard_map/reduce_sum | solution.py:31
  564.9 10.1 %all-reduce.1 = f32[2368]{0:T(1024)S(1)} all-reduce(f32[2368]{0:T(1024)S(1)} %subtract_dynamic-update-slice_fusion.6), channel_id=1, replica_groups=mesh['row'=4,'col'=8] {'row'}, use_global_device_ids=true, to_apply=%add.1 | all-reduce | flops 2368 | bytes 18944
  575.0 16.4 %add_reduce_fusion.5 = f32[4736]{0:T(1024)S(1)} fusion(f32[2368,4736]{1,0:T(8,128)} %get-tuple-element.3, f32[2368]{0:T(1024)S(1)} %all-reduce.1), kind=kLoop, calls=%fused_computation.14 | loop fusion | flops 22424960 | bytes 44887808 | tf_op jit(solution)/shard_map/reduce_max | solution.py:14
  595.5 18.4 %exponential_reduce_fusion.5 = f32[4736]{0:T(1024)S(1)} fusion(f32[2368,4736]{1,0:T(8,128)} %get-tuple-element.3, f32[4736]{0:T(1024)S(1)} %add_reduce_fusion.5, f32[2368]{0:T(1024)S(1)} %all-reduce.1), kind=kLoop, calls=%fused_computation.5 | loop fusion | flops 33639808 | bytes 44906752 | tf_op jit(solution)/shard_map/reduce_sum | solution.py:15
  620.6 6.6 all-to-all-done.5
  627.3 33.5 %all-reduce.2 = f32[4736]{0:T(1024)S(1)} all-reduce(f32[4736]{0:T(1024)S(1)} %subtract_dynamic-update-slice_fusion.5), channel_id=1, replica_groups=mesh['row'=4,'col'=8] {'col'}, use_global_device_ids=true, to_apply=%add.2 | all-reduce | flops 4736 | bytes 37888
  660.8 14.8 %add_reduce_fusion.4 = f32[2368]{0:T(1024)S(1)} fusion(f32[2368,4736]{1,0:T(8,128)} %get-tuple-element.3, f32[4736]{0:T(1024)S(1)} %all-reduce.2), kind=kLoop, calls=%fused_computation.13 | loop fusion | flops 22427328 | bytes 44887808 | tf_op jit(solution)/shard_map/reduce_max | solution.py:30
  679.5 15.9 %exponential_reduce_fusion.4 = f32[2368]{0:T(1024)S(1)} fusion(f32[2368,4736]{1,0:T(8,128)} %get-tuple-element.3, f32[2368]{0:T(1024)S(1)} %add_reduce_fusion.4, f32[4736]{0:T(1024)S(1)} %all-reduce.2), kind=kLoop, calls=%fused_computation.4 | loop fusion | flops 33642176 | bytes 44897280 | tf_op jit(solution)/shard_map/reduce_sum | solution.py:31
  703.3 10.1 %all-reduce.3 = f32[2368]{0:T(1024)S(1)} all-reduce(f32[2368]{0:T(1024)S(1)} %subtract_dynamic-update-slice_fusion.4), channel_id=1, replica_groups=mesh['row'=4,'col'=8] {'row'}, use_global_device_ids=true, to_apply=%add.3 | all-reduce | flops 2368 | bytes 18944
  713.4 16.4 %add_reduce_fusion.3 = f32[4736]{0:T(1024)S(1)} fusion(f32[2368,4736]{1,0:T(8,128)} %get-tuple-element.3, f32[2368]{0:T(1024)S(1)} %all-reduce.3), kind=kLoop, calls=%fused_computation.12 | loop fusion | flops 22424960 | bytes 44887808 | tf_op jit(solution)/shard_map/reduce_max | solution.py:14
  733.9 18.4 %exponential_reduce_fusion.3 = f32[4736]{0:T(1024)S(1)} fusion(f32[2368,4736]{1,0:T(8,128)} %get-tuple-element.3, f32[4736]{0:T(1024)S(1)} %add_reduce_fusion.3, f32[2368]{0:T(1024)S(1)} %all-reduce.3), kind=kLoop, calls=%fused_computation.3 | loop fusion | flops 33639808 | bytes 44906752 | tf_op jit(solution)/shard_map/reduce_sum | solution.py:15
  758.9 6.6 all-to-all-done.9
  765.7 33.5 %all-reduce.4 = f32[4736]{0:T(1024)S(1)} all-reduce(f32[4736]{0:T(1024)S(1)} %subtract_dynamic-update-slice_fusion.3), channel_id=1, replica_groups=mesh['row'=4,'col'=8] {'col'}, use_global_device_ids=true, to_apply=%add.4 | all-reduce | flops 4736 | bytes 37888
  799.1 14.8 %add_reduce_fusion.2 = f32[2368]{0:T(1024)S(1)} fusion(f32[2368,4736]{1,0:T(8,128)} %get-tuple-element.3, f32[4736]{0:T(1024)S(1)} %all-reduce.4), kind=kLoop, calls=%fused_computation.11 | loop fusion | flops 22427328 | bytes 44887808 | tf_op jit(solution)/shard_map/reduce_max | solution.py:30
  817.8 15.9 %exponential_reduce_fusion.2 = f32[2368]{0:T(1024)S(1)} fusion(f32[2368,4736]{1,0:T(8,128)} %get-tuple-element.3, f32[2368]{0:T(1024)S(1)} %add_reduce_fusion.2, f32[4736]{0:T(1024)S(1)} %all-reduce.4), kind=kLoop, calls=%fused_computation.2 | loop fusion | flops 33642176 | bytes 44897280 | tf_op jit(solution)/shard_map/reduce_sum | solution.py:31
  841.6 10.1 %all-reduce.5 = f32[2368]{0:T(1024)S(1)} all-reduce(f32[2368]{0:T(1024)S(1)} %subtract_dynamic-update-slice_fusion.2), channel_id=1, replica_groups=mesh['row'=4,'col'=8] {'row'}, use_global_device_ids=true, to_apply=%add.5 | all-reduce | flops 2368 | bytes 18944
  851.7 16.4 %add_reduce_fusion.1 = f32[4736]{0:T(1024)S(1)} fusion(f32[2368,4736]{1,0:T(8,128)} %get-tuple-element.3, f32[2368]{0:T(1024)S(1)} %all-reduce.5), kind=kLoop, calls=%fused_computation.10 | loop fusion | flops 22424960 | bytes 44887808 | tf_op jit(solution)/shard_map/reduce_max | solution.py:14
  872.5 18.4 %exponential_reduce_fusion.1 = f32[4736]{0:T(1024)S(1)} fusion(f32[2368,4736]{1,0:T(8,128)} %get-tuple-element.3, f32[4736]{0:T(1024)S(1)} %add_reduce_fusion.1, f32[2368]{0:T(1024)S(1)} %all-reduce.5), kind=kLoop, calls=%fused_computation.1 | loop fusion | flops 33639808 | bytes 44906752 | tf_op jit(solution)/shard_map/reduce_sum | solution.py:15
  897.3 6.6 all-to-all-done.13
  904.0 33.5 %all-reduce.6 = f32[4736]{0:T(1024)S(1)} all-reduce(f32[4736]{0:T(1024)S(1)} %subtract_dynamic-update-slice_fusion.1), channel_id=1, replica_groups=mesh['row'=4,'col'=8] {'col'}, use_global_device_ids=true, to_apply=%add.6 | all-reduce | flops 4736 | bytes 37888
  937.5 14.8 %add_reduce_fusion = f32[2368]{0:T(1024)S(1)} fusion(f32[2368,4736]{1,0:T(8,128)} %get-tuple-element.3, f32[4736]{0:T(1024)S(1)} %all-reduce.6), kind=kLoop, calls=%fused_computation.9 | loop fusion | flops 22427328 | bytes 44887808 | tf_op jit(solution)/shard_map/reduce_max | solution.py:30
  956.2 15.9 %exponential_reduce_fusion = f32[2368]{0:T(1024)S(1)} fusion(f32[2368,4736]{1,0:T(8,128)} %get-tuple-element.3, f32[2368]{0:T(1024)S(1)} %add_reduce_fusion, f32[4736]{0:T(1024)S(1)} %all-reduce.6), kind=kLoop, calls=%fused_computation | loop fusion | flops 33642176 | bytes 44897280 | tf_op jit(solution)/shard_map/reduce_sum | solution.py:31
  980.0 10.7 %all-reduce.7 = f32[2368]{0:T(1024)} all-reduce(f32[2368]{0:T(1024)S(1)} %subtract_dynamic-update-slice_fusion), channel_id=1, replica_groups=mesh['row'=4,'col'=8] {'row'}, use_global_device_ids=true, to_apply=%add.7 | all-reduce | flops 2368 | bytes 18944
  (101 shorter events, 128.0 us)
Async XLA Ops:
  7.2 377.3 %all-gather.2.cloned.1.call-start = ((), (), s32[]{:S(2)}) async-start(), calls=%async_computation.16 | async-start | bytes 21823488 | tf_op jit(solution)/shard_map/all_gather | solution.py:54
  7.9 29.9 %collective-permute-start = (bf16[512,2368]{0,1:T(8,128)(2,1)}, bf16[512,2368]{0,1:T(8,128)(2,1)S(1)}, u32[]{:S(2)}, u32[]{:S(2)}) collective-permute-start(bf16[512,2368]{0,1:T(8,128)(2,1)} %param.3), channel_id=1, source_target_pairs={{0,8},{8,16},{16,24},{24,0},{1,9},{9,17},{17,25},{25,1},{2,10},{10... | collective-permute-start | bytes 7274504 | tf_op jit(solution)/shard_map/ppermute | solution.py:48
  37.8 29.1 %collective-permute-start.1 = (bf16[512,2368]{0,1:T(8,128)(2,1)S(1)}, bf16[512,2368]{0,1:T(8,128)(2,1)}, u32[]{:S(2)}, u32[]{:S(2)}) collective-permute-start(bf16[512,2368]{0,1:T(8,128)(2,1)S(1)} %collective-permute-done), channel_id=1, source_target_pairs={{0,8},{8,16},{16,24},{24,0},{1,9},{9,17},{17,25},{25,1},{2,10},{10... | collective-permute-start | bytes 7274504 | tf_op jit(solution)/shard_map/ppermute | solution.py:48
  66.9 29.3 %collective-permute-start.2 = (bf16[512,2368]{0,1:T(8,128)(2,1)}, bf16[512,2368]{0,1:T(8,128)(2,1)}, u32[]{:S(2)}, u32[]{:S(2)}) collective-permute-start(bf16[512,2368]{0,1:T(8,128)(2,1)} %collective-permute-done.1), channel_id=1, source_target_pairs={{0,8},{8,16},{16,24},{24,0},{1,9},{9,17},{17,25},{25,1},{2,10},{10... | collective-permute-start | bytes 7274504 | tf_op jit(solution)/shard_map/ppermute | solution.py:48
  452.6 29.3 %copy-start.2 = (u32[32]{0:T(128)S(1)}, u32[32]{0:T(128)}, u32[]{:S(2)}) copy-start(u32[32]{0:T(128)} %constant.51) | copy-start | bytes 388
  453.3 22.6 %all-to-all-start = ((f32[8,1,592]{2,1,0:T(1,128)}), f32[8,1,592]{2,1,0:T(1,128)S(1)}, u32[]{:S(2)}, u32[]{:S(2)}) async-start(f32[8,1,592]{2,1,0:T(1,128)} %all_to_all.128), calls=%async_computation | async-start | bytes 40960 | tf_op jit(solution)/shard_map/all_to_all | solution.py:18
  476.0 12.6 %all-to-all-start.1 = ((f32[8,1,592]{2,1,0:T(1,128)}), f32[8,1,592]{2,1,0:T(1,128)S(1)}, u32[]{:S(2)}, u32[]{:S(2)}) async-start(f32[8,1,592]{2,1,0:T(1,128)} %all_to_all.130), calls=%async_computation.1 | async-start | bytes 40960 | tf_op jit(solution)/shard_map/all_to_all | solution.py:21
  522.2 38.8 %copy-start.1 = (u32[32]{0:T(128)S(1)}, u32[32]{0:T(128)}, u32[]{:S(2)}) copy-start(u32[32]{0:T(128)} %constant.56) | copy-start | bytes 388
  537.7 20.0 %all-to-all-start.2 = ((f32[4,1,592]{2,1,0:T(1,128)}), f32[4,1,592]{2,1,0:T(1,128)S(1)}, u32[]{:S(2)}, u32[]{:S(2)}) async-start(f32[4,1,592]{2,1,0:T(1,128)} %all_to_all.134), calls=%async_computation.2 | async-start | bytes 20480 | tf_op jit(solution)/shard_map/all_to_all | solution.py:34
  557.7 7.0 all-to-all-start.3
  592.2 22.5 %all-to-all-start.4 = ((f32[8,1,592]{2,1,0:T(1,128)}), f32[8,1,592]{2,1,0:T(1,128)S(1)}, u32[]{:S(2)}, u32[]{:S(2)}) async-start(f32[8,1,592]{2,1,0:T(1,128)} %all_to_all.140), calls=%async_computation.4 | async-start | bytes 40960 | tf_op jit(solution)/shard_map/all_to_all | solution.py:18
  614.6 12.5 %all-to-all-start.5 = ((f32[8,1,592]{2,1,0:T(1,128)}), f32[8,1,592]{2,1,0:T(1,128)S(1)}, u32[]{:S(2)}, u32[]{:S(2)}) async-start(f32[8,1,592]{2,1,0:T(1,128)} %all_to_all.142), calls=%async_computation.5 | async-start | bytes 40960 | tf_op jit(solution)/shard_map/all_to_all | solution.py:21
  676.2 19.8 %all-to-all-start.6 = ((f32[4,1,592]{2,1,0:T(1,128)}), f32[4,1,592]{2,1,0:T(1,128)S(1)}, u32[]{:S(2)}, u32[]{:S(2)}) async-start(f32[4,1,592]{2,1,0:T(1,128)} %all_to_all.146), calls=%async_computation.6 | async-start | bytes 20480 | tf_op jit(solution)/shard_map/all_to_all | solution.py:34
  696.0 7.1 all-to-all-start.7
  730.5 22.5 %all-to-all-start.8 = ((f32[8,1,592]{2,1,0:T(1,128)}), f32[8,1,592]{2,1,0:T(1,128)S(1)}, u32[]{:S(2)}, u32[]{:S(2)}) async-start(f32[8,1,592]{2,1,0:T(1,128)} %all_to_all.152), calls=%async_computation.8 | async-start | bytes 40960 | tf_op jit(solution)/shard_map/all_to_all | solution.py:18
  753.0 12.5 %all-to-all-start.9 = ((f32[8,1,592]{2,1,0:T(1,128)}), f32[8,1,592]{2,1,0:T(1,128)S(1)}, u32[]{:S(2)}, u32[]{:S(2)}) async-start(f32[8,1,592]{2,1,0:T(1,128)} %all_to_all.154), calls=%async_computation.9 | async-start | bytes 40960 | tf_op jit(solution)/shard_map/all_to_all | solution.py:21
  814.6 19.8 %all-to-all-start.10 = ((f32[4,1,592]{2,1,0:T(1,128)}), f32[4,1,592]{2,1,0:T(1,128)S(1)}, u32[]{:S(2)}, u32[]{:S(2)}) async-start(f32[4,1,592]{2,1,0:T(1,128)} %all_to_all.158), calls=%async_computation.10 | async-start | bytes 20480 | tf_op jit(solution)/shard_map/all_to_all | solution.py:34
  834.4 7.1 all-to-all-start.11
  868.9 22.7 %all-to-all-start.12 = ((f32[8,1,592]{2,1,0:T(1,128)}), f32[8,1,592]{2,1,0:T(1,128)S(1)}, u32[]{:S(2)}, u32[]{:S(2)}) async-start(f32[8,1,592]{2,1,0:T(1,128)} %all_to_all.164), calls=%async_computation.12 | async-start | bytes 40960 | tf_op jit(solution)/shard_map/all_to_all | solution.py:18
  891.6 12.3 %all-to-all-start.13 = ((f32[8,1,592]{2,1,0:T(1,128)}), f32[8,1,592]{2,1,0:T(1,128)S(1)}, u32[]{:S(2)}, u32[]{:S(2)}) async-start(f32[8,1,592]{2,1,0:T(1,128)} %all_to_all.166), calls=%async_computation.13 | async-start | bytes 40960 | tf_op jit(solution)/shard_map/all_to_all | solution.py:21
  937.5 34.6 %copy-start = (f32[4736]{0:T(1024)}, f32[4736]{0:T(1024)S(1)}, u32[]{:S(2)}) copy-start(f32[4736]{0:T(1024)S(1)} %all-reduce.6) | copy-start | bytes 56836
  953.0 19.8 %all-to-all-start.14 = ((f32[4,1,592]{2,1,0:T(1,128)}), f32[4,1,592]{2,1,0:T(1,128)S(1)}, u32[]{:S(2)}, u32[]{:S(2)}) async-start(f32[4,1,592]{2,1,0:T(1,128)} %all_to_all.170), calls=%async_computation.14 | async-start | bytes 20480 | tf_op jit(solution)/shard_map/all_to_all | solution.py:34
  972.8 7.1 all-to-all-start.15
Sparse Core Ops, SparseCore 0:
  9.5 374.9 all-gather.1
